TPU v7x, 32 devices: a 4x2x2 block of a 4x4x8 slice. The times are simulated.
32 devices in a mesh: dp: 4 (over y, z), tp: 8 (over x, core).
Axes of the slice: x: 4, y: 2, z: 2, core: 2. Of those that a mesh axis runs over, the one named last changes fastest.
The devices are a block of a 4x4x8 slice.
Arguments:
- ids: int32 [64, 256], P('dp'), parts along dimension 0
- E: bfloat16 [4096, 4096], P(None, 'tp')
- g: bfloat16 [4096], replicated
- W: bfloat16 [4096, 6144], P(None, 'tp')
- du: bfloat16 [64, 256, 6144], P('dp', None, 'tp'), parts along dimension 0
- dres: bfloat16 [64, 256, 4096], P('dp', 'tp'), parts along dimension 0
Outputs:
- output 1: bfloat16 [64, 256, 6144], P('dp', None, 'tp'), parts along dimension 0
- output 2: bfloat16 [64, 256, 4096], P('dp', 'tp'), parts along dimension 0
- output 3: float32 [16384, 4096], P('dp', 'tp'), parts along dimension 0
- output 4: float32 [16384, 6144], P('dp', 'tp'), parts along dimension 0
- output 5: float32 [16384], P('dp'), parts along dimension 0
There are 4 independent parts. A program takes and returns all parts, laid end to end along the dimension named above; an argument that names none is the same for every part.
All inputs are finite; a program needn't handle non-finite values.
Results may differ from a plain program's by a relative error of at most 0.00617823.
Values are sent between devices in bfloat16 or wider.
A program may use at most 768 MiB of HBM per device.

v0:
```python
import jax
import jax.numpy as jnp
from jax import lax
from jax.sharding import PartitionSpec as P

EPS = 1e-6


def solution(mesh):
    G = mesh.shape['tp']

    def body(ids, E, g, W, du, dres):
        K, T = ids.shape
        D = g.shape[0]
        TL = T // G
        r = lax.axis_index('tp')
        gf = g.astype(jnp.float32)
        dE = jnp.zeros(E.shape, jnp.float32)
        dW = jnp.zeros(W.shape, jnp.float32)
        dg = jnp.zeros((D,), jnp.float32)
        us = []
        xs = []
        for m in range(K):
            xl = jnp.take(E, ids[m], axis=0)
            x = lax.all_gather(xl, 'tp', axis=1, tiled=True)
            xf = x.astype(jnp.float32)
            rs = lax.rsqrt(jnp.mean(xf * xf, axis=-1, keepdims=True) + EPS)
            nh = xf * rs
            n = (nh * gf).astype(jnp.bfloat16)
            us.append(jnp.dot(n, W, preferred_element_type=jnp.float32).astype(jnp.bfloat16))
            dW = dW + jnp.einsum('td,tf->df', n, du[m], preferred_element_type=jnp.float32)
            dnp = jnp.einsum('tf,df->td', du[m], W, preferred_element_type=jnp.float32).astype(jnp.bfloat16)
            dnr = lax.all_to_all(dnp, 'tp', 0, 0, tiled=True)
            dn = jnp.sum(dnr.reshape(G, TL, D).astype(jnp.float32), axis=0)
            xs.append(lax.dynamic_slice_in_dim(x, r * TL, TL, axis=0))
            nhr = lax.dynamic_slice_in_dim(nh, r * TL, TL, axis=0)
            rsr = lax.dynamic_slice_in_dim(rs, r * TL, TL, axis=0)
            gdn = gf * dn
            dx = dres[m].astype(jnp.float32) + rsr * (gdn - nhr * jnp.mean(nhr * gdn, axis=-1, keepdims=True))
            dg = dg + jnp.sum(dn * nhr, axis=0)
            dxw = lax.all_to_all(dx.astype(jnp.bfloat16), 'tp', 1, 0, tiled=True)
            dE = dE.at[ids[m]].add(dxw.astype(jnp.float32))
        dg = lax.psum(dg, 'tp')
        return jnp.stack(us), jnp.stack(xs), dE, dW, dg

    return jax.shard_map(
        body,
        mesh=mesh,
        in_specs=(P('dp', None), P(None, 'tp'), P(), P(None, 'tp'), P('dp', None, 'tp'), P('dp', 'tp', None)),
        out_specs=(P('dp', None, 'tp'), P('dp', 'tp', None), P('dp', 'tp'), P('dp', 'tp'), P('dp')),
        check_vma=False,
    )
```

profile of v0, /device:TPU:81, one launch (start us, length us, event | category | flops | bytes accessed | tf_op | source)
XLA Modules:
  0.0 1313.0 jit_solution(9413636498335016581)
XLA Ops:
  52.8 6.1 convolution_convert_fusion.2
  71.0 28.3 %all-to-all-done.26 = bf16[8,32,4096]{2,1,0:T(8,128)(2,1)S(1)} async-done(((bf16[8,32,4096]{2,1,0:T(8,128)(2,1)}), bf16[8,32,4096]{2,1,0:T(8,128)(2,1)S(1)}, u32[]{:S(2)}, u32[]{:S(2)}) %all-to-all-start.26) | async-done | bytes 2097184 | tf_op jit(solution)/shard_map/all_to_all | solution.py:33
  109.6 6.1 convolution_convert_fusion.4
  115.6 23.7 %all-to-all-done.24 = bf16[8,32,4096]{2,1,0:T(8,128)(2,1)} async-done(((bf16[8,32,4096]{2,1,0:T(8,128)(2,1)}), bf16[8,32,4096]{2,1,0:T(8,128)(2,1)}, u32[]{:S(2)}, u32[]{:S(2)}) %all-to-all-start.24) | async-done | bytes 2097184 | tf_op jit(solution)/shard_map/all_to_all | solution.py:33
  144.7 6.1 convolution_convert_fusion.5
  150.8 25.8 %all-to-all-done.22 = bf16[8,32,4096]{2,1,0:T(8,128)(2,1)} async-done(((bf16[8,32,4096]{2,1,0:T(8,128)(2,1)}), bf16[8,32,4096]{2,1,0:T(8,128)(2,1)}, u32[]{:S(2)}, u32[]{:S(2)}) %all-to-all-start.22) | async-done | bytes 2097184 | tf_op jit(solution)/shard_map/all_to_all | solution.py:33
  186.7 6.1 convolution_convert_fusion.6
  192.8 18.8 %all-to-all-done.20 = bf16[8,32,4096]{2,1,0:T(8,128)(2,1)} async-done(((bf16[8,32,4096]{2,1,0:T(8,128)(2,1)}), bf16[8,32,4096]{2,1,0:T(8,128)(2,1)}, u32[]{:S(2)}, u32[]{:S(2)}) %all-to-all-start.20) | async-done | bytes 2097184 | tf_op jit(solution)/shard_map/all_to_all | solution.py:33
  211.6 6.1 all-to-all-start.18
  217.7 6.1 convolution_convert_fusion.7
  223.7 28.4 %all-to-all-done.18 = bf16[8,32,4096]{2,1,0:T(8,128)(2,1)} async-done(((bf16[8,32,4096]{2,1,0:T(8,128)(2,1)}), bf16[8,32,4096]{2,1,0:T(8,128)(2,1)}, u32[]{:S(2)}, u32[]{:S(2)}) %all-to-all-start.18) | async-done | bytes 2097184 | tf_op jit(solution)/shard_map/all_to_all | solution.py:33
  262.3 6.1 convolution_convert_fusion.8
  268.4 23.7 %all-to-all-done.16 = bf16[8,32,4096]{2,1,0:T(8,128)(2,1)} async-done(((bf16[8,32,4096]{2,1,0:T(8,128)(2,1)}), bf16[8,32,4096]{2,1,0:T(8,128)(2,1)}, u32[]{:S(2)}, u32[]{:S(2)}) %all-to-all-start.16) | async-done | bytes 2097184 | tf_op jit(solution)/shard_map/all_to_all | solution.py:33
  297.4 6.1 convolution_convert_fusion.9
  303.5 25.8 %all-to-all-done.14 = bf16[8,32,4096]{2,1,0:T(8,128)(2,1)} async-done(((bf16[8,32,4096]{2,1,0:T(8,128)(2,1)}), bf16[8,32,4096]{2,1,0:T(8,128)(2,1)}, u32[]{:S(2)}, u32[]{:S(2)}) %all-to-all-start.14) | async-done | bytes 2097184 | tf_op jit(solution)/shard_map/all_to_all | solution.py:33
  339.2 6.1 convolution_convert_fusion.10
  345.3 18.6 %all-to-all-done.12 = bf16[8,32,4096]{2,1,0:T(8,128)(2,1)} async-done(((bf16[8,32,4096]{2,1,0:T(8,128)(2,1)}), bf16[8,32,4096]{2,1,0:T(8,128)(2,1)}, u32[]{:S(2)}, u32[]{:S(2)}) %all-to-all-start.12) | async-done | bytes 2097184 | tf_op jit(solution)/shard_map/all_to_all | solution.py:33
  363.9 6.1 all-to-all-start.10
  370.0 6.1 convolution_convert_fusion.11
  376.1 28.4 %all-to-all-done.10 = bf16[8,32,4096]{2,1,0:T(8,128)(2,1)} async-done(((bf16[8,32,4096]{2,1,0:T(8,128)(2,1)}), bf16[8,32,4096]{2,1,0:T(8,128)(2,1)}, u32[]{:S(2)}, u32[]{:S(2)}) %all-to-all-start.10) | async-done | bytes 2097184 | tf_op jit(solution)/shard_map/all_to_all | solution.py:33
  414.6 6.1 convolution_convert_fusion.12
  420.7 23.7 %all-to-all-done.8 = bf16[8,32,4096]{2,1,0:T(8,128)(2,1)} async-done(((bf16[8,32,4096]{2,1,0:T(8,128)(2,1)}), bf16[8,32,4096]{2,1,0:T(8,128)(2,1)}, u32[]{:S(2)}, u32[]{:S(2)}) %all-to-all-start.8) | async-done | bytes 2097184 | tf_op jit(solution)/shard_map/all_to_all | solution.py:33
  449.7 6.1 convolution_convert_fusion.13
  455.7 20.1 %all-to-all-done.6 = bf16[8,32,4096]{2,1,0:T(8,128)(2,1)} async-done(((bf16[8,32,4096]{2,1,0:T(8,128)(2,1)}), bf16[8,32,4096]{2,1,0:T(8,128)(2,1)}, u32[]{:S(2)}, u32[]{:S(2)}) %all-to-all-start.6) | async-done | bytes 2097184 | tf_op jit(solution)/shard_map/all_to_all | solution.py:33
  486.2 6.1 convolution_convert_fusion.14
  492.3 23.5 %all-to-all-done.4 = bf16[8,32,4096]{2,1,0:T(8,128)(2,1)} async-done(((bf16[8,32,4096]{2,1,0:T(8,128)(2,1)}), bf16[8,32,4096]{2,1,0:T(8,128)(2,1)}, u32[]{:S(2)}, u32[]{:S(2)}) %all-to-all-start.4) | async-done | bytes 2097184 | tf_op jit(solution)/shard_map/all_to_all | solution.py:33
  521.0 6.1 convolution_convert_fusion.15
  527.1 20.1 %all-to-all-done.2 = bf16[8,32,4096]{2,1,0:T(8,128)(2,1)} async-done(((bf16[8,32,4096]{2,1,0:T(8,128)(2,1)}), bf16[8,32,4096]{2,1,0:T(8,128)(2,1)}, u32[]{:S(2)}, u32[]{:S(2)}) %all-to-all-start.2) | async-done | bytes 2097184 | tf_op jit(solution)/shard_map/all_to_all | solution.py:33
  557.3 6.1 convolution_convert_fusion
  563.4 23.7 %all-to-all-done = bf16[8,32,4096]{2,1,0:T(8,128)(2,1)} async-done(((bf16[8,32,4096]{2,1,0:T(8,128)(2,1)}), bf16[8,32,4096]{2,1,0:T(8,128)(2,1)}, u32[]{:S(2)}, u32[]{:S(2)}) %all-to-all-start) | async-done | bytes 2097184 | tf_op jit(solution)/shard_map/all_to_all | solution.py:33
  593.0 6.1 convolution_convert_fusion.1
  758.8 7.3 fusion.64
  766.1 6.7 fusion.63
  772.9 6.6 fusion.62
  779.5 6.7 fusion.61
  786.2 6.6 fusion.60
  792.8 6.6 fusion.59
  799.5 6.8 fusion.58
  806.2 6.7 fusion.57
  812.9 6.7 fusion.56
  819.6 6.7 fusion.55
  826.3 6.7 fusion.54
  832.9 6.6 fusion.53
  839.6 8.0 fusion.52
  847.5 7.6 fusion.51
  855.1 7.7 fusion.50
  909.1 62.1 %add_add_fusion = f32[4096,768]{1,0:T(8,128)} fusion(f32[4096,768]{1,0:T(8,128)} %fusion.64, f32[4096,768]{1,0:T(8,128)} %fusion.63, f32[4096,768]{1,0:T(8,128)} %fusion.62, f32[4096,768]{1,0:T(8,128)} %fusion.61, f32[4096,768]{1,0:T(8,128)} %fusion.60, f32[4096,768]{1,0:T(8,128)} %fusion.59, f32[4096,768]{1,0:T(8,128)} %fusion.58, ...), kind=kOutput, calls=%fused_computation.32 | convolution fusion | flops 1661992960 | bytes 203834368 | tf_op jit(solution)/shard_map/td,tf->df/dot_general | solution.py:31
  1135.4 23.0 %psum.7 = f32[4096]{0:T(1024)} all-reduce(f32[4096]{0:T(1024)S(1)} %add_add_fusion.1), channel_id=1, replica_groups=mesh['dp'=4,'tp'=8] {'tp'}, use_global_device_ids=true, to_apply=%region_80.82 | all-reduce | flops 4096 | bytes 32768 | tf_op jit(solution)/shard_map/psum | solution.py:43
  1159.4 6.1 scatter_custom_fusion
  1166.6 9.0 scatter_fusion
  1175.7 8.8 scatter_fusion.1
  1184.5 8.8 scatter_fusion.2
  1194.4 8.8 scatter_fusion.3
  1203.3 8.9 scatter_fusion.4
  1212.2 8.8 scatter_fusion.5
  1222.0 8.8 scatter_fusion.6
  1231.9 8.8 scatter_fusion.7
  1240.8 9.1 scatter_fusion.8
  1250.9 8.8 scatter_fusion.9
  1260.7 8.8 scatter_fusion.10
  1269.6 8.8 scatter_fusion.11
  1278.5 8.8 scatter_fusion.12
  1288.3 8.8 scatter_fusion.13
  1297.2 8.8 scatter_fusion.14
  (489 shorter events, 533.2 us)
Async XLA Ops:
  7.2 643.1 %all-gather.41.cloned.1.call-start = ((), (), s32[]{:S(2)}) async-start(), calls=%async_computation.44 | async-start | bytes 2359296 | tf_op jit(solution)/shard_map/all_gather | solution.py:25
  13.1 639.3 %all-gather.45.cloned.1.call-start = ((), (), s32[]{:S(2)}) async-start(), calls=%async_computation.46 | async-start | bytes 2359296 | tf_op jit(solution)/shard_map/all_gather | solution.py:25
  18.1 636.6 %all-gather.37.cloned.1.call-start = ((), (), s32[]{:S(2)}) async-start(), calls=%async_computation.42 | async-start | bytes 2359296 | tf_op jit(solution)/shard_map/all_gather | solution.py:25
  23.0 633.9 %all-gather.33.cloned.1.call-start = ((), (), s32[]{:S(2)}) async-start(), calls=%async_computation.40 | async-start | bytes 2359296 | tf_op jit(solution)/shard_map/all_gather | solution.py:25
  28.0 631.1 %all-gather.29.cloned.1.call-start = ((), (), s32[]{:S(2)}) async-start(), calls=%async_computation.38 | async-start | bytes 2359296 | tf_op jit(solution)/shard_map/all_gather | solution.py:25
  32.9 628.3 %all-gather.25.cloned.1.call-start = ((), (), s32[]{:S(2)}) async-start(), calls=%async_computation.36 | async-start | bytes 2359296 | tf_op jit(solution)/shard_map/all_gather | solution.py:25
  37.8 625.6 %all-gather.21.cloned.1.call-start = ((), (), s32[]{:S(2)}) async-start(), calls=%async_computation.34 | async-start | bytes 2359296 | tf_op jit(solution)/shard_map/all_gather | solution.py:25
  42.7 622.8 %all-gather.17.cloned.1.call-start = ((), (), s32[]{:S(2)}) async-start(), calls=%async_computation.32 | async-start | bytes 2359296 | tf_op jit(solution)/shard_map/all_gather | solution.py:25
  47.9 619.9 %all-gather.43.cloned.1.call-start = ((), (), s32[]{:S(2)}) async-start(), calls=%async_computation.45 | async-start | bytes 2359296 | tf_op jit(solution)/shard_map/all_gather | solution.py:25
  58.9 40.4 %all-to-all-start.26 = ((bf16[8,32,4096]{2,1,0:T(8,128)(2,1)}), bf16[8,32,4096]{2,1,0:T(8,128)(2,1)S(1)}, u32[]{:S(2)}, u32[]{:S(2)}) async-start(bf16[8,32,4096]{2,1,0:T(8,128)(2,1)} %bitcast.483), calls=%async_computation.26 | async-start | bytes 4194304 | tf_op jit(solution)/shard_map/all_to_all | solution.py:33
  99.3 40.1 %all-to-all-start.24 = ((bf16[8,32,4096]{2,1,0:T(8,128)(2,1)}), bf16[8,32,4096]{2,1,0:T(8,128)(2,1)}, u32[]{:S(2)}, u32[]{:S(2)}) async-start(bf16[8,32,4096]{2,1,0:T(8,128)(2,1)} %bitcast.470), calls=%async_computation.24 | async-start | bytes 4194304 | tf_op jit(solution)/shard_map/all_to_all | solution.py:33
  104.7 565.2 %all-gather.47.cloned.1.call-start = ((), (), s32[]{:S(2)}) async-start(), calls=%async_computation.47 | async-start | bytes 2359296 | tf_op jit(solution)/shard_map/all_gather | solution.py:25
  139.4 37.2 %all-to-all-start.22 = ((bf16[8,32,4096]{2,1,0:T(8,128)(2,1)}), bf16[8,32,4096]{2,1,0:T(8,128)(2,1)}, u32[]{:S(2)}, u32[]{:S(2)}) async-start(bf16[8,32,4096]{2,1,0:T(8,128)(2,1)} %bitcast.477), calls=%async_computation.22 | async-start | bytes 4194304 | tf_op jit(solution)/shard_map/all_to_all | solution.py:33
  176.5 35.0 %all-to-all-start.20 = ((bf16[8,32,4096]{2,1,0:T(8,128)(2,1)}), bf16[8,32,4096]{2,1,0:T(8,128)(2,1)}, u32[]{:S(2)}, u32[]{:S(2)}) async-start(bf16[8,32,4096]{2,1,0:T(8,128)(2,1)} %bitcast.471), calls=%async_computation.20 | async-start | bytes 4194304 | tf_op jit(solution)/shard_map/all_to_all | solution.py:33
  181.5 490.7 %all-gather.39.cloned.1.call-start = ((), (), s32[]{:S(2)}) async-start(), calls=%async_computation.43 | async-start | bytes 2359296 | tf_op jit(solution)/shard_map/all_gather | solution.py:25
  211.6 40.6 %all-to-all-start.18 = ((bf16[8,32,4096]{2,1,0:T(8,128)(2,1)}), bf16[8,32,4096]{2,1,0:T(8,128)(2,1)}, u32[]{:S(2)}, u32[]{:S(2)}) async-start(bf16[8,32,4096]{2,1,0:T(8,128)(2,1)} %bitcast.478), calls=%async_computation.18 | async-start | bytes 4194304 | tf_op jit(solution)/shard_map/all_to_all | solution.py:33
  252.2 39.9 %all-to-all-start.16 = ((bf16[8,32,4096]{2,1,0:T(8,128)(2,1)}), bf16[8,32,4096]{2,1,0:T(8,128)(2,1)}, u32[]{:S(2)}, u32[]{:S(2)}) async-start(bf16[8,32,4096]{2,1,0:T(8,128)(2,1)} %bitcast.472), calls=%async_computation.16 | async-start | bytes 4194304 | tf_op jit(solution)/shard_map/all_to_all | solution.py:33
  257.5 416.9 %all-gather.35.cloned.1.call-start = ((), (), s32[]{:S(2)}) async-start(), calls=%async_computation.41 | async-start | bytes 2359296 | tf_op jit(solution)/shard_map/all_gather | solution.py:25
  292.1 37.2 %all-to-all-start.14 = ((bf16[8,32,4096]{2,1,0:T(8,128)(2,1)}), bf16[8,32,4096]{2,1,0:T(8,128)(2,1)}, u32[]{:S(2)}, u32[]{:S(2)}) async-start(bf16[8,32,4096]{2,1,0:T(8,128)(2,1)} %bitcast.479), calls=%async_computation.14 | async-start | bytes 4194304 | tf_op jit(solution)/shard_map/all_to_all | solution.py:33
  329.3 34.6 %all-to-all-start.12 = ((bf16[8,32,4096]{2,1,0:T(8,128)(2,1)}), bf16[8,32,4096]{2,1,0:T(8,128)(2,1)}, u32[]{:S(2)}, u32[]{:S(2)}) async-start(bf16[8,32,4096]{2,1,0:T(8,128)(2,1)} %bitcast.473), calls=%async_computation.12 | async-start | bytes 4194304 | tf_op jit(solution)/shard_map/all_to_all | solution.py:33
  334.2 342.3 %all-gather.31.cloned.1.call-start = ((), (), s32[]{:S(2)}) async-start(), calls=%async_computation.39 | async-start | bytes 2359296 | tf_op jit(solution)/shard_map/all_gather | solution.py:25
  363.9 40.7 %all-to-all-start.10 = ((bf16[8,32,4096]{2,1,0:T(8,128)(2,1)}), bf16[8,32,4096]{2,1,0:T(8,128)(2,1)}, u32[]{:S(2)}, u32[]{:S(2)}) async-start(bf16[8,32,4096]{2,1,0:T(8,128)(2,1)} %bitcast.480), calls=%async_computation.10 | async-start | bytes 4194304 | tf_op jit(solution)/shard_map/all_to_all | solution.py:33
  404.6 39.9 %all-to-all-start.8 = ((bf16[8,32,4096]{2,1,0:T(8,128)(2,1)}), bf16[8,32,4096]{2,1,0:T(8,128)(2,1)}, u32[]{:S(2)}, u32[]{:S(2)}) async-start(bf16[8,32,4096]{2,1,0:T(8,128)(2,1)} %bitcast.474), calls=%async_computation.8 | async-start | bytes 4194304 | tf_op jit(solution)/shard_map/all_to_all | solution.py:33
  409.8 269.0 %all-gather.27.cloned.1.call-start = ((), (), s32[]{:S(2)}) async-start(), calls=%async_computation.37 | async-start | bytes 2359296 | tf_op jit(solution)/shard_map/all_gather | solution.py:25
  444.4 31.4 %all-to-all-start.6 = ((bf16[8,32,4096]{2,1,0:T(8,128)(2,1)}), bf16[8,32,4096]{2,1,0:T(8,128)(2,1)}, u32[]{:S(2)}, u32[]{:S(2)}) async-start(bf16[8,32,4096]{2,1,0:T(8,128)(2,1)} %bitcast.481), calls=%async_computation.6 | async-start | bytes 4194304 | tf_op jit(solution)/shard_map/all_to_all | solution.py:33
  475.9 39.9 %all-to-all-start.4 = ((bf16[8,32,4096]{2,1,0:T(8,128)(2,1)}), bf16[8,32,4096]{2,1,0:T(8,128)(2,1)}, u32[]{:S(2)}, u32[]{:S(2)}) async-start(bf16[8,32,4096]{2,1,0:T(8,128)(2,1)} %bitcast.475), calls=%async_computation.4 | async-start | bytes 4194304 | tf_op jit(solution)/shard_map/all_to_all | solution.py:33
  481.2 199.9 %all-gather.23.cloned.1.call-start = ((), (), s32[]{:S(2)}) async-start(), calls=%async_computation.35 | async-start | bytes 2359296 | tf_op jit(solution)/shard_map/all_gather | solution.py:25
  515.8 31.4 %all-to-all-start.2 = ((bf16[8,32,4096]{2,1,0:T(8,128)(2,1)}), bf16[8,32,4096]{2,1,0:T(8,128)(2,1)}, u32[]{:S(2)}, u32[]{:S(2)}) async-start(bf16[8,32,4096]{2,1,0:T(8,128)(2,1)} %bitcast.482), calls=%async_computation.2 | async-start | bytes 4194304 | tf_op jit(solution)/shard_map/all_to_all | solution.py:33
  547.2 40.0 %all-to-all-start = ((bf16[8,32,4096]{2,1,0:T(8,128)(2,1)}), bf16[8,32,4096]{2,1,0:T(8,128)(2,1)}, u32[]{:S(2)}, u32[]{:S(2)}) async-start(bf16[8,32,4096]{2,1,0:T(8,128)(2,1)} %bitcast.476), calls=%async_computation | async-start | bytes 4194304 | tf_op jit(solution)/shard_map/all_to_all | solution.py:33
  552.5 130.7 %all-gather.19.cloned.1.call-start = ((), (), s32[]{:S(2)}) async-start(), calls=%async_computation.33 | async-start | bytes 2359296 | tf_op jit(solution)/shard_map/all_gather | solution.py:25
  563.4 28.9 %copy-start.54 = (s32[16,256]{1,0:T(8,128)S(1)}, s32[16,256]{1,0:T(8,128)}, u32[]{:S(2)}) copy-start(s32[16,256]{1,0:T(8,128)} %param.8) | copy-start | bytes 49156
  563.4 29.6 %copy-start.57 = (bf16[4096]{0:T(1024)(128)(2,1)S(1)}, bf16[4096]{0:T(1024)(128)(2,1)}, u32[]{:S(2)}) copy-start(bf16[4096]{0:T(1024)(128)(2,1)} %param.10) | copy-start | bytes 24580
  587.1 31.4 %all-to-all-start.30 = ((bf16[8,32,4096]{2,1,0:T(8,128)(2,1)}), bf16[8,32,4096]{2,1,0:T(8,128)(2,1)}, u32[]{:S(2)}, u32[]{:S(2)}) async-start(bf16[8,32,4096]{2,1,0:T(8,128)(2,1)} %bitcast.468), calls=%async_computation.30 | async-start | bytes 4194304 | tf_op jit(solution)/shard_map/all_to_all | solution.py:33
  618.5 30.7 %all-to-all-start.28 = ((bf16[8,32,4096]{2,1,0:T(8,128)(2,1)}), bf16[8,32,4096]{2,1,0:T(8,128)(2,1)S(1)}, u32[]{:S(2)}, u32[]{:S(2)}) async-start(bf16[8,32,4096]{2,1,0:T(8,128)(2,1)} %bitcast.469), calls=%async_computation.28 | async-start | bytes 4194304 | tf_op jit(solution)/shard_map/all_to_all | solution.py:33
  672.1 36.3 %copy-start.55 = (f32[256]{0:T(256)}, f32[256]{0:T(256)S(1)}, u32[]{:S(2)}) copy-start(f32[256]{0:T(256)S(1)} %add_rsqrt_fusion) | copy-start | bytes 3076
  696.1 276.8 %all-to-all-start.1 = ((bf16[32,8,512]{2,0,1:T(8,128)(2,1)}), bf16[32,8,512]{2,0,1:T(8,128)(2,1)}, u32[]{:S(2)}, u32[]{:S(2)}) async-start(bf16[32,8,512]{2,0,1:T(8,128)(2,1)} %bitcast.450), calls=%async_computation.1 | async-start | bytes 524288 | tf_op jit(solution)/shard_map/all_to_all | solution.py:41
  745.3 13.5 %slice-start = ((s8[6291456]{0:T(1024)(128)(4,1)}), s8[2097152]{0:T(1024)(128)(4,1)S(1)}, s32[]{:S(2)}) async-start(s8[6291456]{0:T(1024)(128)(4,1)} %bitcast.451), calls=%async_computation.48 | async-start | bytes 4194304
  862.8 11.2 slice-start.2
  972.8 11.2 all-to-all-start.5
  984.0 10.9 all-to-all-start.7
  994.9 10.9 all-to-all-start.11
  1005.7 10.9 all-to-all-start.13
  1017.3 10.9 all-to-all-start.25
  1028.1 10.9 all-to-all-start.27
  1039.0 11.5 all-to-all-start.21
  1044.1 90.4 %copy-start.45 = (f32[4096]{0:T(1024)S(1)}, f32[4096]{0:T(1024)}, u32[]{:S(2)}) copy-start(f32[4096]{0:T(1024)} %get-tuple-element.8) | copy-start | bytes 49156
  1044.1 90.4 %copy-start.46 = (f32[4096]{0:T(1024)S(1)}, f32[4096]{0:T(1024)}, u32[]{:S(2)}) copy-start(f32[4096]{0:T(1024)} %get-tuple-element.14) | copy-start | bytes 49156
  1044.1 90.4 %copy-start.47 = (f32[4096]{0:T(1024)S(1)}, f32[4096]{0:T(1024)}, u32[]{:S(2)}) copy-start(f32[4096]{0:T(1024)} %get-tuple-element.92) | copy-start | bytes 49156
  1044.1 90.4 %copy-start.48 = (f32[4096]{0:T(1024)S(1)}, f32[4096]{0:T(1024)}, u32[]{:S(2)}) copy-start(f32[4096]{0:T(1024)} %get-tuple-element.94) | copy-start | bytes 49156
  1044.1 90.4 %copy-start.49 = (f32[4096]{0:T(1024)S(1)}, f32[4096]{0:T(1024)}, u32[]{:S(2)}) copy-start(f32[4096]{0:T(1024)} %get-tuple-element.36) | copy-start | bytes 49156
  1044.1 90.4 %copy-start.50 = (f32[4096]{0:T(1024)S(1)}, f32[4096]{0:T(1024)}, u32[]{:S(2)}) copy-start(f32[4096]{0:T(1024)} %get-tuple-element.56) | copy-start | bytes 49156
  1044.1 90.4 %copy-start.51 = (f32[4096]{0:T(1024)S(1)}, f32[4096]{0:T(1024)}, u32[]{:S(2)}) copy-start(f32[4096]{0:T(1024)} %get-tuple-element.58) | copy-start | bytes 49156
  1044.1 90.4 %copy-start.52 = (f32[4096]{0:T(1024)S(1)}, f32[4096]{0:T(1024)}, u32[]{:S(2)}) copy-start(f32[4096]{0:T(1024)} %get-tuple-element.60) | copy-start | bytes 49156
  1044.1 90.4 %copy-start.53 = (f32[4096]{0:T(1024)S(1)}, f32[4096]{0:T(1024)}, u32[]{:S(2)}) copy-start(f32[4096]{0:T(1024)} %get-tuple-element.62) | copy-start | bytes 49156
  1050.5 11.5 all-to-all-start.29
  1061.9 11.5 all-to-all-start.17
  1073.4 11.5 all-to-all-start.3
  1084.8 11.5 all-to-all-start.9
  1096.3 11.5 all-to-all-start.15
  1107.7 11.5 all-to-all-start.23
  1119.2 10.9 all-to-all-start.19
  1130.0 167.1 %all-to-all-start.31 = ((bf16[32,8,512]{2,0,1:T(8,128)(2,1)}), bf16[32,8,512]{2,0,1:T(8,128)(2,1)S(1)}, u32[]{:S(2)}, u32[]{:S(2)}) async-start(bf16[32,8,512]{2,0,1:T(8,128)(2,1)} %bitcast.500), calls=%async_computation.31 | async-start | bytes 524288 | tf_op jit(solution)/shard_map/all_to_all | solution.py:41
  1184.5 9.8 copy-start.69
  1240.8 10.1 copy-start.63
  (61 other events, 294.8 us)
Sparse Core Ops, SparseCore 0:
  13.3 26.5 all-gather.40
  41.4 22.5 all-gather.44
  65.6 28.9 all-gather.36
  96.0 37.9 all-gather.32
  135.5 28.6 all-gather.28
  165.6 25.2 all-gather.24
  192.5 26.7 all-gather.20
  221.4 28.6 all-gather.16
  251.8 34.9 all-gather.42
  288.2 28.6 all-gather.46
  318.5 25.1 all-gather.38
  345.2 26.9 all-gather.34
  373.8 28.4 all-gather.30
  414.8 29.4 all-gather.26
  486.3 29.4 all-gather.22
  557.4 29.4 all-gather.18
where the time goes:
time: 1330 us; the launch traced here: 1310 us
  waiting for transfers between devices  408 us (31%)
  matrix products  315 us (24%)
  other arithmetic  276 us (21%)
  starting transfers between devices  164 us (12%)
  local copies, waits for them, and re-layouts  111 us (8%)
  blocking collectives  23 us (2%)
  between operations  15.7 us (1%)
    all_to_all x16, waiting for transfers between devices, body(): dnr = lax.all_to_all(dnp, 'tp', 0, 0, tiled=True)  340 us
    dot_general x16, matrix products, body(): jnp.einsum('td,tf->df', n, du[m], preferred_element_type=jnp.float32)  166 us
    scatter-add x16, other arithmetic, body(): dE = dE.at[ids[m]].add(dxw.astype(jnp.float32))  139 us
    dot_general x16, matrix products, body(): jnp.einsum('tf,df->td', du[m], W, preferred_element_type=jnp.float32)  97.3 us
    all_to_all x16, starting transfers between devices, body(): dnr = lax.all_to_all(dnp, 'tp', 0, 0, tiled=True)  86 us
    all_to_all x16, starting transfers between devices, body(): dxw = lax.all_to_all(dx.astype(jnp.bfloat16), 'tp', 1, 0, tiled=True)  76.7 us
    all_to_all x16, waiting for transfers between devices, body(): dxw = lax.all_to_all(dx.astype(jnp.bfloat16), 'tp', 1, 0, tiled=True)  66.8 us
    gather x16, local copies, waits for them, and re-layouts, body(): xl = jnp.take(E, ids[m], axis=0)  63 us
  transfers between devices with their start and end apart: 48, of which 30 were waited for; matrix products, arithmetic and copies ran while one was open for 51% of the time, Pallas kernels for 0%

commit v1 on v0

v1 whole, which is shorter than its diff:
```python
import functools

import jax
import jax.numpy as jnp
from jax import lax
from jax.experimental import pallas as pl
from jax.experimental.pallas import tpu as pltpu
from jax.sharding import PartitionSpec as P

EPS = 1e-6
TM = 512
f32, bf16 = jnp.float32, jnp.bfloat16
MESH = pl.DeviceIdType.MESH


def kernel(G, DN, ids_col, ids_row, g8, E, W, du, dr,
           u_o, x_o, dE_o, dW_o, dg_o,
           xbuf, dup, drw, dst, pf0, pb, rb, st,
           E_v, W_v, wp_v, dW_v, dE_v, rs_v, acc_v, accu_v, d3_v, drl_v,
           s_loc, s_rcv, sm_v, dg_loc, dg_all, lsem, ssem, rsem):
    C = G // 2
    K, TL, D = dr.shape
    N, FL = du.shape
    V, DL = E.shape
    T = TL * G
    NTILE = N // TM
    MT = TM // T
    r = lax.axis_index('tp')
    k, c = lax.div(r, 2), lax.rem(r, 2)
    mate = r + 1 - 2 * c
    right = lax.rem(r + 2, G)
    left = lax.rem(r + G - 2, G)

    def blk(o, p):
        return lax.rem(k + o, C) * 2 + (c if p == 0 else 1 - c)

    def cols(b, n=DL):
        return pl.ds(pl.multiple_of(b * DL, DL), n)

    used = [0]

    def rcopy(src, dstr, dev):
        i = used[0]
        used[0] += 1
        return pltpu.make_async_remote_copy(
            src_ref=src, dst_ref=dstr, send_sem=ssem.at[i], recv_sem=rsem.at[i],
            device_id={'tp': dev}, device_id_type=MESH)

    sent = []

    def start(cp):
        cp.start()
        sent.append(cp)
        return cp

    barrier = pltpu.get_barrier_semaphore()
    for d in range(1, G):
        pl.semaphore_signal(barrier, inc=1, device_id={'tp': lax.rem(r + d, G)}, device_id_type=MESH)
    pl.semaphore_wait(barrier, G - 1)

    rows = pl.ds(pl.multiple_of(r * TL, TL), TL)
    Kh = K // 2
    dres_in = []
    to_r = start(rcopy(dr.at[pl.ds(0, Kh), :, cols(lax.rem(k + 2, C) * 2, 2 * DL)], dst.at[0], right))
    to_l = start(rcopy(dr.at[pl.ds(Kh, Kh), :, cols(lax.rem(k + 2, C) * 2, 2 * DL)], dst.at[1], left))
    for o in (1, C - 1):
        for p in range(2):
            b = blk(o, p)
            dres_in.append(start(rcopy(dr.at[:, :, cols(b)], drw.at[:, rows, :], b)))
    dup_cp = start(rcopy(du, dup, mate))
    wp_cp = [start(rcopy(W.at[cols(blk(o, 1)), :], wp_v.at[o], mate)) for o in range(C)]
    dres_in.append(start(rcopy(dr.at[:, :, cols(mate)], drw.at[:, rows, :], mate)))

    cE = pltpu.make_async_copy(E, E_v, lsem.at[0])
    cW = pltpu.make_async_copy(W, W_v, lsem.at[1])
    cD = pltpu.make_async_copy(dr.at[:, :, cols(r)], drl_v, lsem.at[2])
    cE.start()
    cW.start()
    cD.start()
    cE.wait()

    NA = 2
    NT = N // NA
    h = NT // 2
    TA = NT // TM

    def gather(step, id_b, xl_b):
        acc_v[...] = jnp.zeros_like(acc_v)

        @pl.loop(0, V // TM)
        def _(v):
            it = lax.broadcasted_iota(jnp.int32, (TM, TM), 1) + v * TM
            oh = jnp.where(id_b[...] == it, 1.0, 0.0).astype(bf16)
            acc_v[...] += jnp.dot(oh, E_v[pl.ds(pl.multiple_of(v * TM, TM), TM), :], preferred_element_type=f32)

        xl_b[...] = acc_v[...].astype(bf16)

    x_first = []
    for i in range(NA):
        pltpu.emit_pipeline(
            gather, grid=(TA,),
            in_specs=[pl.BlockSpec((TM, 1), lambda t, i=i: (t + i * TA, 0))],
            out_specs=[pl.BlockSpec((TM, DL), lambda t, i=i: (t + i * TA, 0))],
            _explicit_indices=True,
        )(ids_col, xbuf.at[0])
        cs = pl.ds(i * NT, NT)
        x_first.append((
            start(rcopy(xbuf.at[0, cs], xbuf.at[6, cs], right)),
            start(rcopy(xbuf.at[0, cs], xbuf.at[2, cs], left)),
            start(rcopy(xbuf.at[0, cs], xbuf.at[1, cs], mate))))

    cD.wait()
    cD2 = pltpu.make_async_copy(drl_v, drw.at[:, rows, :], lsem.at[2])
    cD2.start()
    dW_v[...] = jnp.zeros_like(dW_v)
    dE_v[...] = jnp.zeros_like(dE_v)
    dg_loc[...] = jnp.zeros_like(dg_loc)

    to_r.wait_recv()
    rl = pl.ds(pl.multiple_of(left * TL, TL), TL)
    rr = pl.ds(pl.multiple_of(right * TL, TL), TL)
    for p in range(2):
        q = c if p == 0 else 1 - c
        dres_in.append(start(rcopy(dst.at[0, :, :, pl.ds(pl.multiple_of(q * DL, DL), DL)],
                                   drw.at[pl.ds(0, Kh), rl, :], lax.rem(k + 1, C) * 2 + q)))
    to_l.wait_recv()
    for p in range(2):
        q = c if p == 0 else 1 - c
        dres_in.append(start(rcopy(dst.at[1, :, :, pl.ds(pl.multiple_of(q * DL, DL), DL)],
                                   drw.at[pl.ds(Kh, Kh), rr, :], lax.rem(k + C - 1, C) * 2 + q)))

    cW.wait()
    dup_cp.wait_recv()
    for cp in wp_cp:
        cp.wait_recv()
    nt_dims = (((1,), (1,)), ((), ()))

    def partial(step, du_b, dp_b, p0_b, p_b):
        for o in range(C):
            w = W_v[cols(blk(o, 0)), :]
            a = lax.dot_general(du_b[...], w, nt_dims, preferred_element_type=f32)
            a = a + lax.dot_general(dp_b[...], wp_v[o], nt_dims, preferred_element_type=f32)
            if o == 0:
                p0_b[...] = a
            else:
                p_b[o - 1] = a.astype(bf16)

    tile = lambda t: (t, 0)
    pltpu.emit_pipeline(
        partial, grid=(NTILE,),
        in_specs=[pl.BlockSpec((TM, FL), tile), pl.BlockSpec((TM, FL), tile)],
        out_specs=[pl.BlockSpec((TM, DL), tile), pl.BlockSpec((C - 1, TM, DL), lambda t: (0, t, 0))],
        _explicit_indices=True,
    )(du, dup, pf0, pb)

    x_second, x_mate = [], []
    for i in range(NA):
        fr, fl, _ = x_first[i]
        lo, hi = pl.ds(i * NT, h), pl.ds(i * NT + h, h)
        cs = pl.ds(i * NT, NT)
        fr.wait_recv()
        a = start(rcopy(xbuf.at[6, lo], xbuf.at[4, lo], right))
        m6 = start(rcopy(xbuf.at[6, cs], xbuf.at[7, cs], mate))
        fl.wait_recv()
        b = start(rcopy(xbuf.at[2, hi], xbuf.at[4, hi], left))
        m2 = start(rcopy(xbuf.at[2, cs], xbuf.at[3, cs], mate))
        x_second.append((a, b))
        x_mate.append([m6, m2])

    def dn_send(i):
        t0, n = DN[i]
        lo, hi = pl.ds(t0 * TM, n * TM // 2), pl.ds(t0 * TM + n * TM // 2, n * TM // 2)
        cs = pl.ds(t0 * TM, n * TM)
        return (start(rcopy(pb.at[0, cs], rb.at[2, cs], right)),
                start(rcopy(pb.at[2, cs], rb.at[0, cs], left)),
                start(rcopy(pb.at[1, lo], st.at[lo], right)),
                start(rcopy(pb.at[1, hi], st.at[hi], left)), lo, hi)

    def dn_forward(q):
        a, b, ra, rbk, lo, hi = q
        ra.wait_recv()
        f1 = start(rcopy(st.at[lo], rb.at[1, lo], right))
        rbk.wait_recv()
        f2 = start(rcopy(st.at[hi], rb.at[1, hi], left))
        return a, b, f1, f2

    first = [dn_send(0), dn_send(1)]

    t_dims = (((0,), (0,)), ((), ()))

    def forward(step, i, x_b, du_b, u_b, xo_b):
        t = step.index[0] + i * TA
        rs_v[pl.ds(pl.multiple_of(t * TM, TM), TM), :] = jnp.zeros((TM, 1), f32)
        here = pl.ds(pl.multiple_of(t * TM, TM), TM)

        @pl.loop(0, G)
        def _(j):
            x = x_b[j].astype(f32)
            rs_v[here, :] += jnp.sum(x * x, axis=-1, keepdims=True)

        rs_v[here, :] = lax.rsqrt(rs_v[here, :] / D + EPS)
        accu_v[...] = jnp.zeros_like(accu_v)

        @pl.loop(0, G)
        def _(j):
            p = lax.rem(j, 2)
            b = lax.rem(k + lax.div(j, 2), C) * 2 + c + p - 2 * c * p
            n = ((x_b[j].astype(f32) * rs_v[here, :]) * g8[pl.ds(b, 1), :]).astype(bf16)
            accu_v[...] += jnp.dot(n, W_v[cols(b), :], preferred_element_type=f32)
            dW_v[cols(b), :] += lax.dot_general(n, du_b[...], t_dims, preferred_element_type=f32)
            for m in range(MT):
                xo_b[m, :, cols(b)] = x_b[j, pl.ds(pl.multiple_of(m * T + r * TL, TL), TL), :]

        uf = accu_v[...]
        u_b[...] = uf.astype(bf16)
        s = jnp.sum(uf * du_b[...].astype(f32), axis=-1, keepdims=True)
        s_loc[pl.ds(t, 1), :] = jnp.broadcast_to(s, (TM, 128)).T[0:1, :]

    for i in range(NA):
        a, b = x_second[i]
        lo, hi = pl.ds(i * NT, h), pl.ds(i * NT + h, h)
        a.wait_recv()
        m4a = start(rcopy(xbuf.at[4, lo], xbuf.at[5, lo], mate))
        b.wait_recv()
        m4b = start(rcopy(xbuf.at[4, hi], xbuf.at[5, hi], mate))
        x_first[i][2].wait_recv()
        for cp in x_mate[i]:
            cp.wait_recv()
        m4a.wait_recv()
        m4b.wait_recv()
        at = lambda t, i=i: (t + i * TA, 0)
        pltpu.emit_pipeline(
            lambda step, *refs, i=i: forward(step, i, *refs), grid=(TA,),
            in_specs=[pl.BlockSpec((G, TM, DL), lambda t, i=i: (0, t + i * TA, 0)), pl.BlockSpec((TM, FL), at)],
            out_specs=[pl.BlockSpec((TM, FL), at), pl.BlockSpec((MT, TL, D), lambda t, i=i: (t + i * TA, 0, 0))],
            _explicit_indices=True,
        )(xbuf, du, u_o, x_o)

    cdW = pltpu.make_async_copy(dW_v, dW_o, lsem.at[3])
    cdW.start()
    s_cp = [start(rcopy(s_loc, s_rcv.at[G - d - 1], lax.rem(r + d, G))) for d in range(1, G)]
    done = [dn_forward(first[0])]
    rest = [dn_send(i) for i in range(2, len(DN))]
    for cp in s_cp:
        cp.wait_recv()
    tot = jnp.zeros_like(s_loc)
    for dev in range(G):
        d = lax.rem(dev - r + G, G)
        other = s_rcv[lax.max(d - 1, 0)]
        tot = tot + jnp.where(d == 0, s_loc[...], other)
    sm_v[...] = tot / D
    done.append(dn_forward(first[1]))
    cD2.wait()
    for cp in dres_in:
        cp.wait_recv()

    def backward(step, t0, p0_b, rb_b, xl_b, dr_b):
        t = step.index[0] + t0
        here = pl.ds(pl.multiple_of(t * TM, TM), TM)
        dn = (p0_b[...] + rb_b[0].astype(f32)) + (rb_b[1].astype(f32) + rb_b[2].astype(f32))
        rs = rs_v[here, :]
        s = jnp.broadcast_to(sm_v[pl.ds(t, 1), :], (128, TM)).T[:, 0:1]
        nh = xl_b[...].astype(f32) * rs
        dx = dr_b[...].reshape(TM, DL).astype(f32) + rs * (g8[pl.ds(r, 1), :] * dn - nh * s)
        dg_loc[0:1, :] += jnp.sum(dn * nh, axis=0, keepdims=True)
        hi = dx.astype(bf16)
        e1 = dx - hi.astype(f32)
        md = e1.astype(bf16)
        d3_v[0] = hi
        d3_v[1] = md
        d3_v[2] = (e1 - md.astype(f32)).astype(bf16)

        @pl.loop(0, V // TM)
        def _(v):
            it = lax.broadcasted_iota(jnp.int32, (TM, TM), 0) + v * TM
            oh = jnp.where(ids_row[pl.ds(t, 1), :] == it, 1.0, 0.0).astype(bf16)
            a = jnp.dot(oh, d3_v[0], preferred_element_type=f32)
            a = a + jnp.dot(oh, d3_v[1], preferred_element_type=f32)
            a = a + jnp.dot(oh, d3_v[2], preferred_element_type=f32)
            dE_v[pl.ds(pl.multiple_of(v * TM, TM), TM), :] += a

    for i, (t0, n) in enumerate(DN):
        if i >= 2:
            pass
        a, b, f1, f2 = done[i]
        a.wait_recv()
        b.wait_recv()
        f1.wait_recv()
        f2.wait_recv()
        at = lambda t, t0=t0: (t + t0, 0)
        pltpu.emit_pipeline(
            lambda step, *refs, t0=t0: backward(step, t0, *refs), grid=(n,),
            in_specs=[pl.BlockSpec((TM, DL), at),
                      pl.BlockSpec((C - 1, TM, DL), lambda t, t0=t0: (0, t + t0, 0)),
                      pl.BlockSpec((TM, DL), at),
                      pl.BlockSpec((MT, T, DL), lambda t, t0=t0: (t + t0, 0, 0))],
            out_specs=[],
            _explicit_indices=True,
        )(pf0, rb, xbuf.at[0], drw)
        if i == 0:
            done += [dn_forward(q) for q in rest]

    cdE = pltpu.make_async_copy(dE_v, dE_o, lsem.at[4])
    cdE.start()
    dg_cp = [start(rcopy(dg_loc, dg_all.at[r], lax.rem(r + d, G))) for d in range(1, G)]
    dg_all[r] = dg_loc[...]
    for cp in dg_cp:
        cp.wait_recv()
    cg = pltpu.make_async_copy(dg_all, dg_o, lsem.at[5])
    cg.start()
    cg.wait()
    cdE.wait()
    cdW.wait()
    for cp in sent:
        cp.wait_send()


def solution(mesh):
    G = mesh.shape['tp']

    def body(ids, E, g, W, du, dres):
        K, T = ids.shape
        D = g.shape[0]
        V, DL = E.shape
        FL = W.shape[1]
        TL = T // G
        N = K * T
        C = G // 2
        nt = N // TM
        DN = ((0, nt // 2), (nt // 2, nt // 4), (nt - nt // 4, nt // 8), (nt - nt // 8, nt // 8))
        ncp = 64 + 6 * len(DN)
        S = jax.ShapeDtypeStruct
        anyspec = pl.BlockSpec(memory_space=pl.ANY)
        vspec = pl.BlockSpec(memory_space=pltpu.VMEM)
        outs = pl.pallas_call(
            functools.partial(kernel, G, DN),
            out_shape=[S((N, FL), bf16), S((K, TL, D), bf16), S((V, DL), f32), S((D, FL), f32), S((G, 8, DL), f32),
                       S((G, N, DL), bf16), S((N, FL), bf16), S((K, T, DL), bf16), S((2, K // 2, TL, 2 * DL), bf16),
                       S((N, DL), f32), S((C - 1, N, DL), bf16), S((C - 1, N, DL), bf16), S((N, DL), bf16)],
            in_specs=[anyspec, vspec, vspec, anyspec, anyspec, anyspec, anyspec],
            out_specs=[anyspec] * 13,
            scratch_shapes=[
                pltpu.VMEM((V, DL), bf16),
                pltpu.VMEM((D, FL), bf16),
                pltpu.VMEM((C, DL, FL), bf16),
                pltpu.VMEM((D, FL), f32),
                pltpu.VMEM((V, DL), f32),
                pltpu.VMEM((N, 1), f32),
                pltpu.VMEM((TM, TM), f32),
                pltpu.VMEM((TM, FL), f32),
                pltpu.VMEM((3, TM, DL), bf16),
                pltpu.VMEM((K, TL, DL), bf16),
                pltpu.VMEM((nt, TM), f32),
                pltpu.VMEM((G - 1, nt, TM), f32),
                pltpu.VMEM((nt, TM), f32),
                pltpu.VMEM((8, DL), f32),
                pltpu.VMEM((G, 8, DL), f32),
                pltpu.SemaphoreType.DMA((6,)),
                pltpu.SemaphoreType.DMA((ncp,)),
                pltpu.SemaphoreType.DMA((ncp,)),
            ],
            compiler_params=pltpu.CompilerParams(collective_id=0, has_side_effects=True, vmem_limit_bytes=66000000),
        )(ids.reshape(N, 1), ids.reshape(nt, TM), g.astype(f32).reshape(G, DL), E, W, du.reshape(N, FL), dres)
        u, x, dE, dW, dg = outs[:5]
        return u.reshape(K, T, FL), x, dE, dW, dg[:, 0, :].reshape(D)

    return jax.shard_map(
        body,
        mesh=mesh,
        in_specs=(P('dp', None), P(None, 'tp'), P(), P(None, 'tp'), P('dp', None, 'tp'), P('dp', 'tp', None)),
        out_specs=(P('dp', None, 'tp'), P('dp', 'tp', None), P('dp', 'tp'), P('dp', 'tp'), P('dp')),
        check_vma=False,
    )
```

time: 1330 us -> 438 us (0.33); the launches traced: 1310 us -> 437 us
  waiting for transfers between devices: 408 us -> 0 us
  Pallas kernels: 0 us -> 405 us
  matrix products: 315 us -> 0 us
  other arithmetic: 276 us -> 0 us
  starting transfers between devices: 164 us -> 0 us
  local copies, waits for them, and re-layouts: 111 us -> 31.5 us
  blocking collectives: 23 us -> 0 us
  between operations: 15.7 us -> 0.65 us
    all_to_all x32 -> x0, waiting for transfers between devices: 407 us -> none  [the longest x16 340 us: body(): dnr = lax.all_to_all(dnp, 'tp', 0, 0, tiled=True)]
    pallas_call x0 -> x1, Pallas kernels: none -> 405 us  [body(): pl.pallas_call(functools.partial(kernel, G, DN), out_shape=[S((N, FL), bf...]
    dot_general x48 -> x0, matrix products: 315 us -> none  [the longest x16 166 us: body(): jnp.einsum('td,tf->df', n, du[m], preferred_element_type=jnp.float32)]
    all_to_all x32 -> x0, starting transfers between devices: 163 us -> none  [the longest x16 86 us: body(): dnr = lax.all_to_all(dnp, 'tp', 0, 0, tiled=True)]
    scatter-add x16 -> x0, other arithmetic: 139 us -> none  [body(): dE = dE.at[ids[m]].add(dxw.astype(jnp.float32))]
    reduce_sum x35 -> x0, other arithmetic: 80.4 us -> none  [the longest x16 38.8 us: body(): dn = jnp.sum(dnr.reshape(G, TL, D).astype(jnp.float32), axis=0)]
    gather x16 -> x0, local copies, waits for them, and re-layouts: 63 us -> none  [body(): xl = jnp.take(E, ids[m], axis=0)]
    psum x1 -> x0, blocking collectives: 23 us -> none  [body(): dg = lax.psum(dg, 'tp')]
  transfers between devices with their start and end apart: 48 -> 0, of which waited for: 30 -> 0; matrix products, arithmetic and copies ran while one was open for 51% -> 0% of each run, Pallas kernels for 0% -> 0%
where the time goes in v1:
time: 438 us; the launch traced here: 437 us
  Pallas kernels  405 us (92%)
  local copies, waits for them, and re-layouts  31.5 us (7%)
    pallas_call x1, Pallas kernels, body(): pl.pallas_call(functools.partial(kernel, G, DN), out_shape=[S((N, FL), bf...  405 us
    unnamed x10, local copies, waits for them, and re-layouts  27.4 us

profile of v1, /device:TPU:81, one launch (start us, length us, event | category | flops | bytes accessed | tf_op | source)
XLA Modules:
  0.0 437.0 jit_solution(5978635965389319707)
XLA Ops:
  0.6 1.3 reshape.34.g8
  1.9 0.7 copy.12
  2.7 1.3 reshape.28.ids_row
  4.0 2.0 copy.13
  6.0 404.9 %shard_map.101 = (bf16[4096,768]{1,0:T(8,128)(2,1)}, bf16[16,32,4096]{2,1,0:T(8,128)(2,1)}, f32[4096,512]{1,0:T(8,128)}, f32[4096,768]{1,0:T(8,128)}, f32[8,8,51...) custom-call(s32[4096,1]{1,0:T(8,128)} %bitcast.7, ...), custom_call_target="tpu_custom_call" | custom-call | tf_op jit(solution)/shard_map/pallas_call | solution.py:335
  410.9 1.5 slice.3
  412.4 0.0 copy-start.1
  412.4 6.2 %copy.18 = bf16[16,256,768]{2,1,0:T(8,128)(2,1)} copy(bf16[16,256,768]{2,1,0:T(8,128)(2,1)} %bitcast.8) | data formatting | bytes 12582912
  418.6 0.0 copy-done.1
  418.6 0.0 copy-start
  418.6 2.1 copy.19
  420.7 2.8 copy-done
  423.5 3.4 copy.20
  426.9 10.2 %copy.21 = f32[4096,768]{1,0:T(8,128)} copy(f32[4096,768]{1,0:T(8,128)} %get-tuple-element.23) | data formatting | bytes 25165824
Async XLA Ops:
  412.4 6.2 %copy-start.1 = (bf16[16,32,4096]{2,1,0:T(8,128)(2,1)S(1)}, bf16[16,32,4096]{2,1,0:T(8,128)(2,1)}, u32[]{:S(2)}) copy-start(bf16[16,32,4096]{2,1,0:T(8,128)(2,1)} %get-tuple-element.21) | copy-start | bytes 12582916
  418.6 4.9 %copy-start = (f32[4096,512]{1,0:T(8,128)S(1)}, f32[4096,512]{1,0:T(8,128)}, u32[]{:S(2)}) copy-start(f32[4096,512]{1,0:T(8,128)} %get-tuple-element.22) | copy-start | bytes 25165828

commit v2 on v1

--- a/solution.py
+++ b/solution.py
@@ -9,12 +9,37 @@
 
 EPS = 1e-6
 TM = 512
+AHEAD = 3
+LATE = 1
 f32, bf16 = jnp.float32, jnp.bfloat16
 MESH = pl.DeviceIdType.MESH
 
 
-def kernel(G, DN, ids_col, ids_row, g8, E, W, du, dr,
-           u_o, x_o, dE_o, dW_o, dg_o,
+def id_row(ids, t, n):
+    return jnp.concatenate([ids[pl.ds(t + m, 1), :] for m in range(n)], axis=1)
+
+
+def tail(MT, t0, ids, d3, dg, u, x, dE, dW, u_o, x_o, dE_o, dW_o, dg_o):
+    u_o[...] = u[...]
+    x_o[...] = x[...]
+    dW_o[...] = dW[...]
+    VB = dE.shape[0]
+    NL = d3.shape[1]
+    it = lax.broadcasted_iota(jnp.int32, (VB, NL), 0) + pl.program_id(0) * VB
+    oh = jnp.where(id_row(ids, t0, MT * NL // TM) == it, 1.0, 0.0).astype(bf16)
+    a = jnp.dot(oh, d3[0], preferred_element_type=f32)
+    a = a + jnp.dot(oh, d3[1], preferred_element_type=f32)
+    a = a + jnp.dot(oh, d3[2], preferred_element_type=f32)
+    dE_o[...] = dE[...] + a
+
+    @pl.when(pl.program_id(0) == 0)
+    def _():
+        for b in range(dg.shape[0]):
+            dg_o[0:1, b * dg.shape[2]:(b + 1) * dg.shape[2]] = dg[b, 0:1, :]
+
+
+def kernel(G, AHEAD, LATE, ids, g8, E, W, du, dr,
+           u_o, x_o, dE_o, dW_o, dg_o, d3_o,
            xbuf, dup, drw, dst, pf0, pb, rb, st,
            E_v, W_v, wp_v, dW_v, dE_v, rs_v, acc_v, accu_v, d3_v, drl_v,
            s_loc, s_rcv, sm_v, dg_loc, dg_all, lsem, ssem, rsem):
@@ -84,13 +109,15 @@
     h = NT // 2
     TA = NT // TM
 
-    def gather(step, id_b, xl_b):
+    def gather(step, i, xl_b):
         acc_v[...] = jnp.zeros_like(acc_v)
+        row = id_row(ids, (step.index[0] + i * TA) * MT, MT).astype(f32)
+        id_b = jnp.broadcast_to(row, (128, TM)).T[:, 0:1].astype(jnp.int32)
 
         @pl.loop(0, V // TM)
         def _(v):
             it = lax.broadcasted_iota(jnp.int32, (TM, TM), 1) + v * TM
-            oh = jnp.where(id_b[...] == it, 1.0, 0.0).astype(bf16)
+            oh = jnp.where(id_b == it, 1.0, 0.0).astype(bf16)
             acc_v[...] += jnp.dot(oh, E_v[pl.ds(pl.multiple_of(v * TM, TM), TM), :], preferred_element_type=f32)
 
         xl_b[...] = acc_v[...].astype(bf16)
@@ -98,11 +125,10 @@
     x_first = []
     for i in range(NA):
         pltpu.emit_pipeline(
-            gather, grid=(TA,),
-            in_specs=[pl.BlockSpec((TM, 1), lambda t, i=i: (t + i * TA, 0))],
+            lambda step, xl_b, i=i: gather(step, i, xl_b), grid=(TA,),
             out_specs=[pl.BlockSpec((TM, DL), lambda t, i=i: (t + i * TA, 0))],
             _explicit_indices=True,
-        )(ids_col, xbuf.at[0])
+        )(xbuf.at[0])
         cs = pl.ds(i * NT, NT)
         x_first.append((
             start(rcopy(xbuf.at[0, cs], xbuf.at[6, cs], right)),
@@ -143,13 +169,13 @@
             if o == 0:
                 p0_b[...] = a
             else:
-                p_b[o - 1] = a.astype(bf16)
+                p_b[o - 1, 0] = a.astype(bf16)
 
     tile = lambda t: (t, 0)
     pltpu.emit_pipeline(
         partial, grid=(NTILE,),
         in_specs=[pl.BlockSpec((TM, FL), tile), pl.BlockSpec((TM, FL), tile)],
-        out_specs=[pl.BlockSpec((TM, DL), tile), pl.BlockSpec((C - 1, TM, DL), lambda t: (0, t, 0))],
+        out_specs=[pl.BlockSpec((TM, DL), tile), pl.BlockSpec((C - 1, 1, TM, DL), lambda t: (0, t, 0, 0))],
         _explicit_indices=True,
     )(du, dup, pf0, pb)
 
@@ -167,24 +193,24 @@
         x_second.append((a, b))
         x_mate.append([m6, m2])
 
-    def dn_send(i):
-        t0, n = DN[i]
-        lo, hi = pl.ds(t0 * TM, n * TM // 2), pl.ds(t0 * TM + n * TM // 2, n * TM // 2)
-        cs = pl.ds(t0 * TM, n * TM)
-        return (start(rcopy(pb.at[0, cs], rb.at[2, cs], right)),
-                start(rcopy(pb.at[2, cs], rb.at[0, cs], left)),
-                start(rcopy(pb.at[1, lo], st.at[lo], right)),
-                start(rcopy(pb.at[1, hi], st.at[hi], left)), lo, hi)
-
-    def dn_forward(q):
-        a, b, ra, rbk, lo, hi = q
-        ra.wait_recv()
-        f1 = start(rcopy(st.at[lo], rb.at[1, lo], right))
-        rbk.wait_recv()
-        f2 = start(rcopy(st.at[hi], rb.at[1, hi], left))
-        return a, b, f1, f2
-
-    first = [dn_send(0), dn_send(1)]
+    TH = TM // 2
+    tlo, thi = pl.ds(0, TH), pl.ds(TH, TH)
+    across = []
+    NG = NTILE // 2
+    for q in range(2):
+        gs = pl.ds(q * NG, NG)
+        across.append((start(rcopy(pb.at[1, gs, tlo], st.at[gs, tlo], right)),
+                       start(rcopy(pb.at[1, gs, thi], st.at[gs, thi], left))))
+
+    def dn_send(t):
+        return (start(rcopy(pb.at[0, t], rb.at[2, t], right)),
+                start(rcopy(pb.at[2, t], rb.at[0, t], left)))
+
+    def dn_forward(t):
+        return (start(rcopy(st.at[t, tlo], rb.at[1, t, tlo], right)),
+                start(rcopy(st.at[t, thi], rb.at[1, t, thi], left)))
+
+    near = [dn_send(t) for t in range(AHEAD)]
 
     t_dims = (((0,), (0,)), ((), ()))
 
@@ -239,8 +265,9 @@
     cdW = pltpu.make_async_copy(dW_v, dW_o, lsem.at[3])
     cdW.start()
     s_cp = [start(rcopy(s_loc, s_rcv.at[G - d - 1], lax.rem(r + d, G))) for d in range(1, G)]
-    done = [dn_forward(first[0])]
-    rest = [dn_send(i) for i in range(2, len(DN))]
+    for cp in across[0]:
+        cp.wait_recv()
+    far = [dn_forward(t) for t in range(AHEAD)]
     for cp in s_cp:
         cp.wait_recv()
     tot = jnp.zeros_like(s_loc)
@@ -249,15 +276,16 @@
         other = s_rcv[lax.max(d - 1, 0)]
         tot = tot + jnp.where(d == 0, s_loc[...], other)
     sm_v[...] = tot / D
-    done.append(dn_forward(first[1]))
+    for cp in across[1]:
+        cp.wait_recv()
     cD2.wait()
     for cp in dres_in:
         cp.wait_recv()
 
-    def backward(step, t0, p0_b, rb_b, xl_b, dr_b):
+    def backward(step, t0, p0_b, rb_b, xl_b, dr_b, *late):
         t = step.index[0] + t0
         here = pl.ds(pl.multiple_of(t * TM, TM), TM)
-        dn = (p0_b[...] + rb_b[0].astype(f32)) + (rb_b[1].astype(f32) + rb_b[2].astype(f32))
+        dn = (p0_b[...] + rb_b[0, 0].astype(f32)) + (rb_b[1, 0].astype(f32) + rb_b[2, 0].astype(f32))
         rs = rs_v[here, :]
         s = jnp.broadcast_to(sm_v[pl.ds(t, 1), :], (128, TM)).T[:, 0:1]
         nh = xl_b[...].astype(f32) * rs
@@ -266,42 +294,45 @@
         hi = dx.astype(bf16)
         e1 = dx - hi.astype(f32)
         md = e1.astype(bf16)
-        d3_v[0] = hi
-        d3_v[1] = md
-        d3_v[2] = (e1 - md.astype(f32)).astype(bf16)
+        to = late[0] if late else d3_v
+        to[0] = hi
+        to[1] = md
+        to[2] = (e1 - md.astype(f32)).astype(bf16)
+        if late:
+            return
+
+        row = id_row(ids, t * MT, MT)
 
         @pl.loop(0, V // TM)
         def _(v):
             it = lax.broadcasted_iota(jnp.int32, (TM, TM), 0) + v * TM
-            oh = jnp.where(ids_row[pl.ds(t, 1), :] == it, 1.0, 0.0).astype(bf16)
+            oh = jnp.where(row == it, 1.0, 0.0).astype(bf16)
             a = jnp.dot(oh, d3_v[0], preferred_element_type=f32)
             a = a + jnp.dot(oh, d3_v[1], preferred_element_type=f32)
             a = a + jnp.dot(oh, d3_v[2], preferred_element_type=f32)
             dE_v[pl.ds(pl.multiple_of(v * TM, TM), TM), :] += a
 
-    for i, (t0, n) in enumerate(DN):
-        if i >= 2:
-            pass
-        a, b, f1, f2 = done[i]
-        a.wait_recv()
-        b.wait_recv()
-        f1.wait_recv()
-        f2.wait_recv()
-        at = lambda t, t0=t0: (t + t0, 0)
+    for i in range(NTILE):
+        for cp in near[i] + far[i]:
+            cp.wait_recv()
+        if i + AHEAD < NTILE:
+            near.append(dn_send(i + AHEAD))
+            far.append(dn_forward(i + AHEAD))
+        late = i >= NTILE - LATE
+        at = lambda t, i=i: (t + i, 0)
         pltpu.emit_pipeline(
-            lambda step, *refs, t0=t0: backward(step, t0, *refs), grid=(n,),
+            lambda step, *refs, i=i: backward(step, i, *refs), grid=(1,),
             in_specs=[pl.BlockSpec((TM, DL), at),
-                      pl.BlockSpec((C - 1, TM, DL), lambda t, t0=t0: (0, t + t0, 0)),
+                      pl.BlockSpec((C - 1, 1, TM, DL), lambda t, i=i: (0, t + i, 0, 0)),
                       pl.BlockSpec((TM, DL), at),
-                      pl.BlockSpec((MT, T, DL), lambda t, t0=t0: (t + t0, 0, 0))],
-            out_specs=[],
+                      pl.BlockSpec((MT, T, DL), lambda t, i=i: (t + i, 0, 0))],
+            out_specs=[pl.BlockSpec((3, TM, DL), lambda t, i=i: (0, t + i - (NTILE - LATE), 0))] if late else [],
             _explicit_indices=True,
-        )(pf0, rb, xbuf.at[0], drw)
-        if i == 0:
-            done += [dn_forward(q) for q in rest]
-
-    cdE = pltpu.make_async_copy(dE_v, dE_o, lsem.at[4])
-    cdE.start()
+        )(*([pf0, rb, xbuf.at[0], drw] + ([d3_o] if late else [])))
+        if i == NTILE - LATE - 1:
+            cdE = pltpu.make_async_copy(dE_v, dE_o, lsem.at[4])
+            cdE.start()
+
     dg_cp = [start(rcopy(dg_loc, dg_all.at[r], lax.rem(r + d, G))) for d in range(1, G)]
     dg_all[r] = dg_loc[...]
     for cp in dg_cp:
@@ -327,18 +358,19 @@
         N = K * T
         C = G // 2
         nt = N // TM
-        DN = ((0, nt // 2), (nt // 2, nt // 4), (nt - nt // 4, nt // 8), (nt - nt // 8, nt // 8))
-        ncp = 64 + 6 * len(DN)
+        NL = LATE * TM
+        ncp = 64 + 4 * nt
         S = jax.ShapeDtypeStruct
         anyspec = pl.BlockSpec(memory_space=pl.ANY)
         vspec = pl.BlockSpec(memory_space=pltpu.VMEM)
         outs = pl.pallas_call(
-            functools.partial(kernel, G, DN),
+            functools.partial(kernel, G, AHEAD, LATE),
             out_shape=[S((N, FL), bf16), S((K, TL, D), bf16), S((V, DL), f32), S((D, FL), f32), S((G, 8, DL), f32),
+                       S((3, NL, DL), bf16),
                        S((G, N, DL), bf16), S((N, FL), bf16), S((K, T, DL), bf16), S((2, K // 2, TL, 2 * DL), bf16),
-                       S((N, DL), f32), S((C - 1, N, DL), bf16), S((C - 1, N, DL), bf16), S((N, DL), bf16)],
-            in_specs=[anyspec, vspec, vspec, anyspec, anyspec, anyspec, anyspec],
-            out_specs=[anyspec] * 13,
+                       S((N, DL), f32), S((C - 1, nt, TM, DL), bf16), S((C - 1, nt, TM, DL), bf16), S((nt, TM, DL), bf16)],
+            in_specs=[vspec, vspec, anyspec, anyspec, anyspec, anyspec],
+            out_specs=[anyspec] * 14,
             scratch_shapes=[
                 pltpu.VMEM((V, DL), bf16),
                 pltpu.VMEM((D, FL), bf16),
@@ -360,9 +392,18 @@
                 pltpu.SemaphoreType.DMA((ncp,)),
             ],
             compiler_params=pltpu.CompilerParams(collective_id=0, has_side_effects=True, vmem_limit_bytes=66000000),
-        )(ids.reshape(N, 1), ids.reshape(nt, TM), g.astype(f32).reshape(G, DL), E, W, du.reshape(N, FL), dres)
-        u, x, dE, dW, dg = outs[:5]
-        return u.reshape(K, T, FL), x, dE, dW, dg[:, 0, :].reshape(D)
+        )(ids, g.astype(f32).reshape(G, DL), E, W, du.reshape(N, FL), dres)
+        u, x, dE, dW, dg, d3 = outs[:6]
+        rowblk = lambda n, m: pl.BlockSpec((2 * n // K, m), lambda i: (i, 0))
+        blocks = [rowblk(N, FL), pl.BlockSpec((2, TL, D), lambda i: (i, 0, 0)), rowblk(V, DL), rowblk(D, FL)]
+        u, x, dE, dW, dg = pl.pallas_call(
+            functools.partial(tail, TM // T, (nt - LATE) * TM // T),
+            grid=(K // 2,),
+            out_shape=[S((N, FL), bf16), S((K, TL, D), bf16), S((V, DL), f32), S((D, FL), f32), S((1, D), f32)],
+            in_specs=[vspec, vspec, vspec] + blocks,
+            out_specs=blocks + [pl.BlockSpec((1, D), lambda i: (0, 0))],
+        )(ids, d3, dg, u, x, dE, dW)
+        return u.reshape(K, T, FL), x, dE, dW, dg.reshape(D)
 
     return jax.shard_map(
         body,

time: 438 us -> 406 us (0.927)
  local copies, waits for them, and re-layouts: 31.5 us -> 1.32 us
    unnamed x10 -> x0, local copies, waits for them, and re-layouts: 27.4 us -> none
    pallas_call x1 -> x2, Pallas kernels: 405 us -> 404 us  [the longest x1 379 us: body(): pl.pallas_call(functools.partial(kernel, G, AHEAD, LATE), out_shape=[S((N...]
where the time goes in v2:
time: 406 us
  Pallas kernels  404 us (100%)
    pallas_call x1, Pallas kernels, body(): pl.pallas_call(functools.partial(kernel, G, AHEAD, LATE), out_shape=[S((N...  379 us
    pallas_call x1, Pallas kernels, body(): pl.pallas_call(functools.partial(tail, TM // T, (nt - LATE) * TM // T), g...  25.2 us

profile of v2, /device:TPU:81, one launch (start us, length us, event | category | flops | bytes accessed | tf_op | source)
XLA Modules:
  0.0 406.1 jit_solution(346677550715813445)
XLA Ops:
  0.6 1.3 reshape.30.g8
  1.9 378.7 %shard_map.101 = (bf16[4096,768]{1,0:T(8,128)(2,1)}, bf16[16,32,4096]{2,1,0:T(8,128)(2,1)}, f32[4096,512]{1,0:T(8,128)}, f32[4096,768]{1,0:T(8,128)}, f32[8,8,51...) custom-call(s32[16,256]{1,0:T(8,128)} %ids.3, ...), custom_call_target="tpu_custom_call" | custom-call | tf_op jit(solution)/shard_map/pallas_call | solution.py:366
  380.7 25.2 %shard_map.102 = (bf16[4096,768]{1,0:T(8,128)(2,1)}, bf16[16,32,4096]{2,1,0:T(8,128)(2,1)}, f32[4096,512]{1,0:T(8,128)}, f32[4096,768]{1,0:T(8,128)}, f32[1,4096]{1,0:T(1,128)}) custom-call(s32[16,256]{1,0:T(8,128)} %ids.3, bf16[3,512,512]{2,1,0:T(8,128)(2,1)} %get-tuple-element.16.d3, f32[8,8,512]{2,1,0:T(8,128)} %get-tuple-element.17.dg, ...), custom_call_target="tpu_custom_call" | custom-call | tf_op jit(solution)/shard_map/pallas_call | solution.py:399

commit v3 on v2

--- a/solution.py
+++ b/solution.py
@@ -10,7 +10,8 @@
 EPS = 1e-6
 TM = 512
 AHEAD = 3
-LATE = 1
+VLIM = 41 << 20
+VTAIL = 18 << 20
 f32, bf16 = jnp.float32, jnp.bfloat16
 MESH = pl.DeviceIdType.MESH
 
@@ -19,29 +20,39 @@
     return jnp.concatenate([ids[pl.ds(t + m, 1), :] for m in range(n)], axis=1)
 
 
-def tail(MT, t0, ids, d3, dg, u, x, dE, dW, u_o, x_o, dE_o, dW_o, dg_o):
+def tail(MT, t0, ids, d3, dg, u, x, dE, dW, u_o, x_o, dE_o, dg_o, dW_o, sem):
+    out = pltpu.make_async_copy(dW, dW_o, sem)
+
+    @pl.when(pl.program_id(0) == 0)
+    def _():
+        out.start()
+
     u_o[...] = u[...]
     x_o[...] = x[...]
-    dW_o[...] = dW[...]
-    VB = dE.shape[0]
+    i = pl.program_id(0)
+    VB = dE_o.shape[0]
     NL = d3.shape[1]
-    it = lax.broadcasted_iota(jnp.int32, (VB, NL), 0) + pl.program_id(0) * VB
+    it = lax.broadcasted_iota(jnp.int32, (VB, NL), 0) + i * VB
     oh = jnp.where(id_row(ids, t0, MT * NL // TM) == it, 1.0, 0.0).astype(bf16)
     a = jnp.dot(oh, d3[0], preferred_element_type=f32)
     a = a + jnp.dot(oh, d3[1], preferred_element_type=f32)
     a = a + jnp.dot(oh, d3[2], preferred_element_type=f32)
-    dE_o[...] = dE[...] + a
+    dE_o[...] = dE[pl.ds(pl.multiple_of(i * VB, VB), VB), :] + a
 
     @pl.when(pl.program_id(0) == 0)
     def _():
         for b in range(dg.shape[0]):
             dg_o[0:1, b * dg.shape[2]:(b + 1) * dg.shape[2]] = dg[b, 0:1, :]
 
-
-def kernel(G, AHEAD, LATE, ids, g8, E, W, du, dr,
-           u_o, x_o, dE_o, dW_o, dg_o, d3_o,
+    @pl.when(pl.program_id(0) == pl.num_programs(0) - 1)
+    def _():
+        out.wait()
+
+
+def kernel(G, AHEAD, ids, g8, E, W, du, dr,
+           u_o, x_o, dE_v, dW_v, dg_o, d3_v,
            xbuf, dup, drw, dst, pf0, pb, rb, st,
-           E_v, W_v, wp_v, dW_v, dE_v, rs_v, acc_v, accu_v, d3_v, drl_v,
+           E_v, W_v, wp_v, rs_v, acc_v, accu_v, drl_v,
            s_loc, s_rcv, sm_v, dg_loc, dg_all, lsem, ssem, rsem):
     C = G // 2
     K, TL, D = dr.shape
@@ -262,8 +273,6 @@
             _explicit_indices=True,
         )(xbuf, du, u_o, x_o)
 
-    cdW = pltpu.make_async_copy(dW_v, dW_o, lsem.at[3])
-    cdW.start()
     s_cp = [start(rcopy(s_loc, s_rcv.at[G - d - 1], lax.rem(r + d, G))) for d in range(1, G)]
     for cp in across[0]:
         cp.wait_recv()
@@ -282,7 +291,7 @@
     for cp in dres_in:
         cp.wait_recv()
 
-    def backward(step, t0, p0_b, rb_b, xl_b, dr_b, *late):
+    def backward(step, t0, late, p0_b, rb_b, xl_b, dr_b):
         t = step.index[0] + t0
         here = pl.ds(pl.multiple_of(t * TM, TM), TM)
         dn = (p0_b[...] + rb_b[0, 0].astype(f32)) + (rb_b[1, 0].astype(f32) + rb_b[2, 0].astype(f32))
@@ -294,10 +303,9 @@
         hi = dx.astype(bf16)
         e1 = dx - hi.astype(f32)
         md = e1.astype(bf16)
-        to = late[0] if late else d3_v
-        to[0] = hi
-        to[1] = md
-        to[2] = (e1 - md.astype(f32)).astype(bf16)
+        d3_v[0] = hi
+        d3_v[1] = md
+        d3_v[2] = (e1 - md.astype(f32)).astype(bf16)
         if late:
             return
 
@@ -318,30 +326,23 @@
         if i + AHEAD < NTILE:
             near.append(dn_send(i + AHEAD))
             far.append(dn_forward(i + AHEAD))
-        late = i >= NTILE - LATE
+        late = i == NTILE - 1
         at = lambda t, i=i: (t + i, 0)
         pltpu.emit_pipeline(
-            lambda step, *refs, i=i: backward(step, i, *refs), grid=(1,),
+            lambda step, *refs, i=i, late=late: backward(step, i, late, *refs), grid=(1,),
             in_specs=[pl.BlockSpec((TM, DL), at),
                       pl.BlockSpec((C - 1, 1, TM, DL), lambda t, i=i: (0, t + i, 0, 0)),
                       pl.BlockSpec((TM, DL), at),
                       pl.BlockSpec((MT, T, DL), lambda t, i=i: (t + i, 0, 0))],
-            out_specs=[pl.BlockSpec((3, TM, DL), lambda t, i=i: (0, t + i - (NTILE - LATE), 0))] if late else [],
+            out_specs=[],
             _explicit_indices=True,
-        )(*([pf0, rb, xbuf.at[0], drw] + ([d3_o] if late else [])))
-        if i == NTILE - LATE - 1:
-            cdE = pltpu.make_async_copy(dE_v, dE_o, lsem.at[4])
-            cdE.start()
+        )(pf0, rb, xbuf.at[0], drw)
 
     dg_cp = [start(rcopy(dg_loc, dg_all.at[r], lax.rem(r + d, G))) for d in range(1, G)]
     dg_all[r] = dg_loc[...]
     for cp in dg_cp:
         cp.wait_recv()
-    cg = pltpu.make_async_copy(dg_all, dg_o, lsem.at[5])
-    cg.start()
-    cg.wait()
-    cdE.wait()
-    cdW.wait()
+    dg_o[...] = dg_all[...]
     for cp in sent:
         cp.wait_send()
 
@@ -358,51 +359,51 @@
         N = K * T
         C = G // 2
         nt = N // TM
-        NL = LATE * TM
         ncp = 64 + 4 * nt
         S = jax.ShapeDtypeStruct
         anyspec = pl.BlockSpec(memory_space=pl.ANY)
         vspec = pl.BlockSpec(memory_space=pltpu.VMEM)
         outs = pl.pallas_call(
-            functools.partial(kernel, G, AHEAD, LATE),
-            out_shape=[S((N, FL), bf16), S((K, TL, D), bf16), S((V, DL), f32), S((D, FL), f32), S((G, 8, DL), f32),
-                       S((3, NL, DL), bf16),
+            functools.partial(kernel, G, AHEAD),
+            out_shape=[S((N, FL), bf16), S((K, TL, D), bf16), pltpu.VMEM((V, DL), f32), pltpu.VMEM((D, FL), f32), pltpu.VMEM((G, 8, DL), f32),
+                       pltpu.VMEM((3, TM, DL), bf16),
                        S((G, N, DL), bf16), S((N, FL), bf16), S((K, T, DL), bf16), S((2, K // 2, TL, 2 * DL), bf16),
                        S((N, DL), f32), S((C - 1, nt, TM, DL), bf16), S((C - 1, nt, TM, DL), bf16), S((nt, TM, DL), bf16)],
             in_specs=[vspec, vspec, anyspec, anyspec, anyspec, anyspec],
-            out_specs=[anyspec] * 14,
+            out_specs=[anyspec] * 2 + [vspec] * 4 + [anyspec] * 8,
             scratch_shapes=[
                 pltpu.VMEM((V, DL), bf16),
                 pltpu.VMEM((D, FL), bf16),
                 pltpu.VMEM((C, DL, FL), bf16),
-                pltpu.VMEM((D, FL), f32),
-                pltpu.VMEM((V, DL), f32),
                 pltpu.VMEM((N, 1), f32),
                 pltpu.VMEM((TM, TM), f32),
                 pltpu.VMEM((TM, FL), f32),
-                pltpu.VMEM((3, TM, DL), bf16),
                 pltpu.VMEM((K, TL, DL), bf16),
                 pltpu.VMEM((nt, TM), f32),
                 pltpu.VMEM((G - 1, nt, TM), f32),
                 pltpu.VMEM((nt, TM), f32),
                 pltpu.VMEM((8, DL), f32),
                 pltpu.VMEM((G, 8, DL), f32),
-                pltpu.SemaphoreType.DMA((6,)),
+                pltpu.SemaphoreType.DMA((3,)),
                 pltpu.SemaphoreType.DMA((ncp,)),
                 pltpu.SemaphoreType.DMA((ncp,)),
             ],
-            compiler_params=pltpu.CompilerParams(collective_id=0, has_side_effects=True, vmem_limit_bytes=66000000),
+            compiler_params=pltpu.CompilerParams(collective_id=0, has_side_effects=True, vmem_limit_bytes=VLIM),
         )(ids, g.astype(f32).reshape(G, DL), E, W, du.reshape(N, FL), dres)
         u, x, dE, dW, dg, d3 = outs[:6]
         rowblk = lambda n, m: pl.BlockSpec((2 * n // K, m), lambda i: (i, 0))
-        blocks = [rowblk(N, FL), pl.BlockSpec((2, TL, D), lambda i: (i, 0, 0)), rowblk(V, DL), rowblk(D, FL)]
-        u, x, dE, dW, dg = pl.pallas_call(
-            functools.partial(tail, TM // T, (nt - LATE) * TM // T),
+        blocks = [rowblk(N, FL), pl.BlockSpec((2, TL, D), lambda i: (i, 0, 0)), rowblk(V, DL)]
+        hbm = lambda a: pltpu.with_memory_space_constraint(a, pltpu.HBM)
+        vmem = lambda a: pltpu.with_memory_space_constraint(a, pltpu.VMEM)
+        u, x, dE, dg, dW = pl.pallas_call(
+            functools.partial(tail, TM // T, (nt - 1) * TM // T),
             grid=(K // 2,),
-            out_shape=[S((N, FL), bf16), S((K, TL, D), bf16), S((V, DL), f32), S((D, FL), f32), S((1, D), f32)],
-            in_specs=[vspec, vspec, vspec] + blocks,
-            out_specs=blocks + [pl.BlockSpec((1, D), lambda i: (0, 0))],
-        )(ids, d3, dg, u, x, dE, dW)
+            out_shape=[S((N, FL), bf16), S((K, TL, D), bf16), S((V, DL), f32), S((1, D), f32), S((D, FL), f32)],
+            in_specs=[vspec, vspec, vspec] + blocks[:2] + [vspec, vspec],
+            scratch_shapes=[pltpu.SemaphoreType.DMA],
+            compiler_params=pltpu.CompilerParams(vmem_limit_bytes=VTAIL),
+            out_specs=blocks + [pl.BlockSpec((1, D), lambda i: (0, 0)), anyspec],
+        )(ids, vmem(d3), vmem(dg), hbm(u), hbm(x), vmem(dE), vmem(dW))
         return u.reshape(K, T, FL), x, dE, dW, dg.reshape(D)
 
     return jax.shard_map(

time: 406 us -> 397 us (0.978)
  Pallas kernels: 404 us -> 395 us
    pallas_call x2, Pallas kernels: 404 us -> 395 us  [the longest x1 377 us: body(): pl.pallas_call(functools.partial(kernel, G, AHEAD), out_shape=[S((N, FL),...]
where the time goes in v3:
time: 397 us
  Pallas kernels  395 us (99%)
    pallas_call x1, Pallas kernels, body(): pl.pallas_call(functools.partial(kernel, G, AHEAD), out_shape=[S((N, FL),...  377 us
    pallas_call x1, Pallas kernels, body(): pl.pallas_call(functools.partial(tail, TM // T, (nt - 1) * TM // T), grid...  17.8 us

profile of v3, /device:TPU:81, one launch (start us, length us, event | category | flops | bytes accessed | tf_op | source)
XLA Modules:
  0.0 396.9 jit_solution(1937254858732525888)
XLA Ops:
  0.6 1.3 reshape.30.g8
  1.9 0.0 copy-start
  2.0 377.0 %shard_map.101 = (bf16[4096,768]{1,0:T(8,128)(2,1)}, bf16[16,32,4096]{2,1,0:T(8,128)(2,1)}, f32[4096,512]{1,0:T(8,128)S(1)}, f32[4096,768]{1,0:T(8,128)S(1)}, f3...) custom-call(s32[16,256]{1,0:T(8,128)} %ids.3, ...), custom_call_target="tpu_custom_call" | custom-call | tf_op jit(solution)/shard_map/pallas_call | solution.py:366
  379.0 0.0 copy-done
  379.0 17.8 %shard_map.102 = (bf16[4096,768]{1,0:T(8,128)(2,1)}, bf16[16,32,4096]{2,1,0:T(8,128)(2,1)}, f32[4096,512]{1,0:T(8,128)}, f32[1,4096]{1,0:T(1,128)}, f32[4096,768]{1,0:T(8,128)}) custom-call(s32[16,256]{1,0:T(8,128)S(1)} %copy-done, bf16[3,512,512]{2,1,0:T(8,128)(2,1)S(1)} %get-tuple-element.16.d3, f32[8,8,512]{2,1,0:T(8,128)S(1)} %get-tuple-element.17.dg, ...), custom_call_target="tpu_custom_call" | custom-call | tf_op jit(solution)/shard_map/pallas_call | solution.py:398
Async XLA Ops:
  1.9 377.0 %copy-start = (s32[16,256]{1,0:T(8,128)S(1)}, s32[16,256]{1,0:T(8,128)}, u32[]{:S(2)}) copy-start(s32[16,256]{1,0:T(8,128)} %ids.3) | copy-start | bytes 49156
